TPU v7x, 128 devices: a whole 4x4x4 slice. The times are simulated.
128 devices in a mesh: bits: 128 (over y, z, x, core).
Axes of the slice: x: 4, y: 4, z: 4, core: 2. Of those that a mesh axis runs over, the one named last changes fastest.
Arguments:
- environment: float32 [2, 128, 64, 4096], P(None, 'bits'), may hold values from -6 to 6
- peps: float32 [2, 2, 8, 8, 8, 8], replicated, may hold values from -2 to 2
- operators: float32 [2, 2, 2], replicated, may hold values from -4 to 4
- gauge: float32 [128, 128], replicated, may hold values from -0.5 to 0.5
Outputs:
- absorbed: float32 [2, 128, 262144], P(None, None, 'bits')
- rms: float32 [2], replicated
All inputs are finite; a program needn't handle non-finite values.
Results may differ from a plain program's by a relative error of at most 0.0003.
Values sent between devices are 32-bit elements; how exact they have to be, the bound alone decides.
No kernel may reach another device: no remote copies, remote signals or barrier semaphores. Data moves between devices by JAX's collectives and lax.ppermute only.
A program may use at most 512 MiB of HBM per device.

v0:
```python
import functools
import jax, jax.numpy as jnp
from jax import lax
from jax.experimental import pallas as pl
from jax.experimental.pallas import tpu as pltpu

from jax.sharding import Mesh
from jax.sharding import PartitionSpec as P

BITS = ("bits_0", "bits_1", "bits_2", "bits_3")
EPS = 1e-06
F32, BF16 = jnp.float32, jnp.bfloat16
RS = 136
BS = 72
QS = 65
G = 4

def halves(x):
    hi = x.astype(BF16)
    return hi, (x - hi.astype(F32)).astype(BF16)

def wide(x):
    hi, lo = halves(x)
    return jnp.concatenate([hi, hi, lo], axis=1)

def tall(x):
    hi, lo = halves(x)
    return jnp.concatenate([hi, lo, hi], axis=0)

def mm(w, x):
    return jnp.dot(w, tall(x), preferred_element_type=F32)

def absorb_kernel(env, p, ops, out, x_s, t_s, s_s, bra_w, ket_w):
    lane = lax.broadcasted_iota(jnp.int32, (8, 128), 1)
    low = lane < 64
    for j in range(2):
        pj = p[128 * j:128 * (j + 1), :]
        ket_w[j] = wide(pj.T)
        for a in range(2):
            q = ops[j, a, 0] * pj[:64] + ops[j, a, 1] * pj[64:]
            if j == 0:
                q = jnp.swapaxes(q.reshape(8, 8, 64), 0, 1).reshape(64, 64)
            bra_w[j, 64 * a:64 * (a + 1), :] = wide(q.T)

    def load(kl, _):
        for c in range(32):
            rows = pl.ds(pl.multiple_of(8 * kl, 8), 8)
            v0 = env[0, 0, rows, 128 * c:128 * (c + 1)]
            v1 = env[1, 0, rows, 128 * c:128 * (c + 1)]
            k0, bh = c // 4, c % 4
            at = pl.multiple_of((kl * 8 + k0) * 64 + bh * 16, 16)
            r0 = pltpu.roll(v0, 64, 1)
            r1 = pltpu.roll(v1, 64, 1)
            x_s[pl.ds(at, 8), :] = jnp.where(low, v0, r1)
            x_s[pl.ds(at + 8, 8), :] = jnp.where(low, r0, v1)
        return 0
    lax.fori_loop(0, 8, load, 0)

    def bra(j):
        w = bra_w[j]
        def step(i, _):
            x = jnp.concatenate([x_s[pl.ds(pl.multiple_of((i * G + g) * 64, 64), 64), :] for g in range(G)], axis=1)
            y = mm(w, x)
            for g in range(G):
                for a in range(2):
                    t_s[pl.ds(a * 64 + i * G + g, 64, stride=RS), :] = y[64 * a:64 * (a + 1), 128 * g:128 * (g + 1)]
            return 0
        lax.fori_loop(0, 64 // G, step, 0)

    def ket(j, put):
        w = ket_w[j]
        def step(i, _):
            x = jnp.concatenate([t_s[pl.ds(pl.multiple_of((i * G + g) * RS, 8), 128), :] for g in range(G)], axis=1)
            y = mm(w, x)
            for g in range(G):
                put(i * G + g, y[:, 128 * g:128 * (g + 1)])
            return 0
        lax.fori_loop(0, 64 // G, step, 0)

    bra(0)

    def put0(b, y):
        bd, br = b // 8, b % 8
        for kd in range(8):
            s_s[pl.ds(br * 8 * BS + (bd % 2) * 32 + kd * 4 + bd // 2, 8, stride=BS), :] = y[8 * kd:8 * (kd + 1)]
    ket(0, put0)

    def turn(i, _):
        br, kr = i // 8, i % 8
        z = s_s[pl.ds(pl.multiple_of(i * BS, 8), 64), :].T
        z = jnp.concatenate([z[:64], z[64:]], axis=1)
        for k1 in range(8):
            x_s[pl.ds(pl.multiple_of((kr * 8 + k1) * 64 + br * 8, 8), 8), :] = z[8 * k1:8 * (k1 + 1)]
        return 0
    lax.fori_loop(0, 64, turn, 0)

    bra(1)

    def put1(b, y):
        bd, br = b // 8, b % 8
        for kd in range(8):
            s_s[pl.ds(br * BS + kd * 8 + bd, 8, stride=8 * BS), :] = y[8 * kd:8 * (kd + 1)]
    ket(1, put1)

    def leave(i, _):
        z = s_s[pl.ds(pl.multiple_of(i * BS, 8), 64), :].T
        for e in range(2):
            z_e = jnp.concatenate([z[64 * e:64 * e + 32], z[64 * e + 32:64 * e + 64]], axis=1)
            for h in range(2):
                out[2 * i + h, 16 * e:16 * (e + 1), :] = z_e[16 * h:16 * (h + 1)]
        return 0
    lax.fori_loop(0, 64, leave, 0)

def absorb(env, p, ops):
    vm = pl.BlockSpec(memory_space=pltpu.VMEM)
    return pl.pallas_call(
        absorb_kernel,
        out_shape=jax.ShapeDtypeStruct((128, 32, 128), F32),
        in_specs=[vm, vm, pl.BlockSpec(memory_space=pltpu.SMEM)],
        out_specs=vm,
        scratch_shapes=[
            pltpu.VMEM((4096, 128), F32),
            pltpu.VMEM((64 * RS, 128), F32),
            pltpu.VMEM((64 * BS, 128), F32),
            pltpu.VMEM((2, 128, 192), BF16),
            pltpu.VMEM((2, 64, 384), BF16),
        ],
        compiler_params=pltpu.CompilerParams(vmem_limit_bytes=40 << 20),
        cost_estimate=pl.CostEstimate(flops=2 << 30, bytes_accessed=4 << 20, transcendentals=0),
        name="absorb",
    )(env, p, ops)

def gauge_kernel(r, gm, out, sq, w_s):
    w_s[...] = wide(gm[...])
    lane = lax.broadcasted_iota(jnp.int32, (1, 128), 1)
    row = jnp.zeros((1, 128), F32)
    w = w_s[...]
    for e in range(2):
        tot = jnp.zeros((8, 128), F32)
        for b in range(0, 16, G):
            x = jnp.concatenate([r[pl.ds(e * 16 + b + g, 128, stride=32), :] for g in range(G)], axis=1)
            y = mm(w, x)
            out[e, :, 128 * b:128 * (b + G)] = y
            q = y * y
            q = q.reshape(16, 8, 128 * G).sum(0)
            for g in range(G):
                tot = tot + q[:, 128 * g:128 * (g + 1)]
        row = jnp.where(lane == e, jnp.sum(tot), row)
    sq[...] = jnp.broadcast_to(row[None], (128, 1, 128))

def gauge(r, gm):
    vm = pl.BlockSpec(memory_space=pltpu.VMEM)
    return pl.pallas_call(
        gauge_kernel,
        out_shape=(jax.ShapeDtypeStruct((2, 128, 2048), F32), jax.ShapeDtypeStruct((128, 1, 128), F32)),
        in_specs=[vm, vm],
        out_specs=(vm, vm),
        scratch_shapes=[pltpu.VMEM((128, 384), BF16)],
        compiler_params=pltpu.CompilerParams(vmem_limit_bytes=40 << 20),
        cost_estimate=pl.CostEstimate(flops=1 << 29, bytes_accessed=4 << 20, transcendentals=0),
        name="gauge",
    )(r.reshape(4096, 128), gm)

def scale_kernel(entries, x, sums, out, rms):
    total = jnp.sum(sums[...], axis=(0, 1)).reshape(1, 128)
    lane = lax.broadcasted_iota(jnp.int32, (1, 128), 1)
    for e in range(2):
        mean = jnp.sum(jnp.where(lane == e, total, 0.0), axis=1, keepdims=True) / entries
        at = pl.ds(pl.multiple_of(pl.program_id(0) * 16, 16), 16)
        out[e] = x[e, at, :] * lax.rsqrt(mean + EPS)
        @pl.when(pl.program_id(0) == 0)
        def _():
            rms[e] = jnp.sqrt(mean)[0, 0]

def scale(x, sums, entries):
    vm = pl.BlockSpec(memory_space=pltpu.VMEM)
    return pl.pallas_call(
        functools.partial(scale_kernel, entries),
        grid=(8,),
        out_shape=(jax.ShapeDtypeStruct((2, 128, 2048), F32), jax.ShapeDtypeStruct((2,), F32)),
        in_specs=[vm, vm],
        out_specs=(pl.BlockSpec((2, 16, 2048), lambda i: (0, i, 0)), pl.BlockSpec(memory_space=pltpu.SMEM)),
        compiler_params=pltpu.CompilerParams(vmem_limit_bytes=40 << 20),
        cost_estimate=pl.CostEstimate(flops=1 << 19, bytes_accessed=4 << 20, transcendentals=0),
        name="scale",
    )(x, sums)

def body(environment, peps, operators, gauge_matrix):
    blocks = absorb(environment, peps.reshape(256, 64), operators)
    merged = lax.all_to_all(blocks, BITS, 0, 0, tiled=True)
    gauged, sums = gauge(merged, gauge_matrix)
    sums = lax.all_to_all(sums, BITS, 0, 0, tiled=True)
    entries = gauged.shape[1] * gauged.shape[2] * lax.axis_size(BITS)
    return scale(gauged, sums, entries)


def solution(mesh):
    torus = Mesh(mesh.devices.reshape(4, 4, 4, 2), BITS)
    in_specs = (P(None, BITS, None, None), P(), P(), P())
    out_specs = (P(None, None, BITS), P())
    return jax.shard_map(body, mesh=torus, in_specs=in_specs, out_specs=out_specs, check_vma=False)
```

profile of v0, /device:TPU:1, one launch (start us, length us, event | category | flops | bytes accessed | tf_op | source)
XLA Modules:
  0.0 103.3 jit_solution(11780067799214704701)
XLA Ops:
  0.6 1.5 %reshape.12.p = f32[256,64]{1,0:T(8,128)S(1)} reshape(f32[2,2,8,8,8,8]{5,4,3,2,1,0:T(8,128)} %param.5) | data formatting | bytes 131072 | tf_op jit(solution)/shard_map/reshape | solution.py:189
  2.2 0.0 copy-start.1
  2.2 1.6 %copy-done.1 = f32[2,1,64,4096]{3,2,1,0:T(8,128)S(1)} copy-done((f32[2,1,64,4096]{3,2,1,0:T(8,128)S(1)}, f32[2,1,64,4096]{3,2,1,0:T(8,128)}, u32[]{:S(2)}) %copy-start.1) | copy-done | bytes 2097176
  3.8 0.0 copy-start.2
  3.8 0.7 copy-done.2
  4.4 36.9 %absorb.1 = f32[128,32,128]{2,1,0:T(8,128)S(1)} custom-call(f32[2,1,64,4096]{3,2,1,0:T(8,128)S(1)} %copy-done.1, f32[256,64]{1,0:T(8,128)S(1)} %reshape.12.p, f32[2,2,2]{2,1,0:T(2,128)S(1)} %copy-done.2), custom_call_target="tpu_custom_call" | custom-call | flops 2147483648 | bytes 4194304 | tf_op jit(solution)/shard_map/absorb/pallas_call | solution.py:116
  41.3 0.0 copy-start
  41.3 41.7 %all_to_all.10 = f32[128,32,128]{2,1,0:T(8,128)S(1)} all-to-all(f32[128,32,128]{2,1,0:T(8,128)S(1)} %absorb.1), channel_id=1, replica_groups=mesh['bits_0'=4,'bits_1'=4,'bits_2'=4,'bits_3'=2] {'bits_0','bits_1','bi..., dimensions={0} | all-to-all | bytes 4194304 | tf_op jit(solution)/shard_map/all_to_all | solution.py:190
  83.1 0.0 copy-done
  83.1 2.0 %gauge.1 = (f32[2,128,2048]{2,1,0:T(8,128)S(1)}, f32[128,1,128]{2,1,0:T(1,128)S(1)}) custom-call(f32[4096,128]{1,0:T(8,128)S(1)} %bitcast.3, f32[128,128]{1,0:T(8,128)S(1)} %copy-done), custom_call_target="tpu_custom_call" | custom-call | flops 536870912 | bytes 4194304 | tf_op jit(solution)/shard_map/gauge/pallas_call | solution.py:153
  85.0 13.7 %all_to_all.11.sums = f32[128,1,128]{2,1,0:T(1,128)S(1)} all-to-all(f32[128,1,128]{2,1,0:T(1,128)S(1)} %get-tuple-element.5), channel_id=1, replica_groups=mesh['bits_0'=4,'bits_1'=4,'bits_2'=4,'bits_3'=2] {'bits_0','bits_1','bi..., dimensions={0} | all-to-all | bytes 131072 | tf_op jit(solution)/shard_map/all_to_all | solution.py:192
  98.8 4.5 %scale.1 = (f32[2,128,2048]{2,1,0:T(8,128)}, f32[2]{0:T(128)}) custom-call(f32[2,128,2048]{2,1,0:T(8,128)S(1)} %get-tuple-element.4.x, f32[128,1,128]{2,1,0:T(1,128)S(1)} %all_to_all.11.sums), custom_call_target="tpu_custom_call" | custom-call | flops 524288 | bytes 4194304 | tf_op jit(solution)/shard_map/scale/pallas_call | solution.py:177
Async XLA Ops:
  2.2 1.6 %copy-start.1 = (f32[2,1,64,4096]{3,2,1,0:T(8,128)S(1)}, f32[2,1,64,4096]{3,2,1,0:T(8,128)}, u32[]{:S(2)}) copy-start(f32[2,1,64,4096]{3,2,1,0:T(8,128)} %env.1) | copy-start | bytes 6291460
  3.8 0.7 copy-start.2
  41.3 41.8 %copy-start = (f32[128,128]{1,0:T(8,128)S(1)}, f32[128,128]{1,0:T(8,128)}, u32[]{:S(2)}) copy-start(f32[128,128]{1,0:T(8,128)} %gm.1) | copy-start | bytes 196612
where the time goes:
time: 104 us; the launch traced here: 103 us
  blocking collectives  55.5 us (53%)
  Pallas kernels  43.4 us (42%)
  local copies, waits for them, and re-layouts  3.8 us (4%)
    all_to_all x1, blocking collectives, body(): merged = lax.all_to_all(blocks, BITS, 0, 0, tiled=True)  41.7 us
    pallas_call x1, Pallas kernels, absorb(): pl.pallas_call(absorb_kernel, out_shape=jax.ShapeDtypeStruct((128, 32, 12...  36.9 us
    all_to_all x1, blocking collectives, body(): sums = lax.all_to_all(sums, BITS, 0, 0, tiled=True)  13.7 us
    pallas_call x1, Pallas kernels, scale(): pl.pallas_call(functools.partial(scale_kernel, entries), grid=(8,), out_s...  4.54 us
    unnamed x6, local copies, waits for them, and re-layouts  2.27 us

commit v1 on v0

--- a/solution.py
+++ b/solution.py
@@ -10,106 +10,129 @@
 BITS = ("bits_0", "bits_1", "bits_2", "bits_3")
 EPS = 1e-06
 F32, BF16 = jnp.float32, jnp.bfloat16
-RS = 136
-BS = 72
-QS = 65
+UB = 4
+UK = 4
+UT = 8
+RS = 132
+BS = 68
 G = 4
+
 
 def halves(x):
     hi = x.astype(BF16)
     return hi, (x - hi.astype(F32)).astype(BF16)
 
+
 def wide(x):
     hi, lo = halves(x)
     return jnp.concatenate([hi, hi, lo], axis=1)
 
+
 def tall(x):
     hi, lo = halves(x)
     return jnp.concatenate([hi, lo, hi], axis=0)
 
+
 def mm(w, x):
     return jnp.dot(w, tall(x), preferred_element_type=F32)
 
+
+def loop(count, unroll, step):
+    def several(i, carry):
+        for u in range(unroll):
+            step(i * unroll + u)
+        return carry
+
+    lax.fori_loop(0, count // unroll, several, 0)
+
+
+def swap(a, b, low):
+    return jnp.where(low, a, pltpu.roll(b, 64, 1)), jnp.where(low, pltpu.roll(a, 64, 1), b)
+
+
 def absorb_kernel(env, p, ops, out, x_s, t_s, s_s, bra_w, ket_w):
-    lane = lax.broadcasted_iota(jnp.int32, (8, 128), 1)
-    low = lane < 64
+    low = lax.broadcasted_iota(jnp.int32, (8, 128), 1) < 64
     for j in range(2):
-        pj = p[128 * j:128 * (j + 1), :]
+        pj = p[128 * j : 128 * (j + 1), :]
         ket_w[j] = wide(pj.T)
         for a in range(2):
             q = ops[j, a, 0] * pj[:64] + ops[j, a, 1] * pj[64:]
             if j == 0:
                 q = jnp.swapaxes(q.reshape(8, 8, 64), 0, 1).reshape(64, 64)
-            bra_w[j, 64 * a:64 * (a + 1), :] = wide(q.T)
-
-    def load(kl, _):
-        for c in range(32):
-            rows = pl.ds(pl.multiple_of(8 * kl, 8), 8)
-            v0 = env[0, 0, rows, 128 * c:128 * (c + 1)]
-            v1 = env[1, 0, rows, 128 * c:128 * (c + 1)]
-            k0, bh = c // 4, c % 4
-            at = pl.multiple_of((kl * 8 + k0) * 64 + bh * 16, 16)
-            r0 = pltpu.roll(v0, 64, 1)
-            r1 = pltpu.roll(v1, 64, 1)
-            x_s[pl.ds(at, 8), :] = jnp.where(low, v0, r1)
-            x_s[pl.ds(at + 8, 8), :] = jnp.where(low, r0, v1)
-        return 0
-    lax.fori_loop(0, 8, load, 0)
-
-    def bra(j):
-        w = bra_w[j]
-        def step(i, _):
-            x = jnp.concatenate([x_s[pl.ds(pl.multiple_of((i * G + g) * 64, 64), 64), :] for g in range(G)], axis=1)
-            y = mm(w, x)
+            bra_w[j, 64 * a : 64 * (a + 1), :] = wide(q.T)
+
+    def first(at):
+        kl, k0 = at // 8, at % 8
+        rows = pl.ds(pl.multiple_of(8 * kl, 8), 8)
+        pieces = []
+        for c in range(4):
+            lanes = pl.ds(pl.multiple_of(k0 * 512 + 128 * c, 128), 128)
+            pieces += swap(env[0, 0, rows, lanes], env[1, 0, rows, lanes], low)
+        return jnp.concatenate(pieces, axis=0)
+
+    def second(at):
+        return x_s[pl.ds(pl.multiple_of(at * 64, 64), 64), :]
+
+    def bra(j, get):
+        def step(i):
+            y = mm(bra_w[j], jnp.concatenate([get(i * G + g) for g in range(G)], axis=1))
             for g in range(G):
                 for a in range(2):
-                    t_s[pl.ds(a * 64 + i * G + g, 64, stride=RS), :] = y[64 * a:64 * (a + 1), 128 * g:128 * (g + 1)]
-            return 0
-        lax.fori_loop(0, 64 // G, step, 0)
+                    t_s[pl.ds(a * 64 + i * G + g, 64, stride=RS), :] = y[64 * a : 64 * (a + 1), 128 * g : 128 * (g + 1)]
+
+        loop(64 // G, UB, step)
 
     def ket(j, put):
-        w = ket_w[j]
-        def step(i, _):
-            x = jnp.concatenate([t_s[pl.ds(pl.multiple_of((i * G + g) * RS, 8), 128), :] for g in range(G)], axis=1)
-            y = mm(w, x)
+        def step(i):
+            x = jnp.concatenate([t_s[pl.ds((i * G + g) * RS, 128), :] for g in range(G)], axis=1)
+            y = mm(ket_w[j], x)
             for g in range(G):
-                put(i * G + g, y[:, 128 * g:128 * (g + 1)])
-            return 0
-        lax.fori_loop(0, 64 // G, step, 0)
-
-    bra(0)
+                put(i * G + g, y[:, 128 * g : 128 * (g + 1)])
+
+        loop(64 // G, UK, step)
+
+    bra(0, first)
 
     def put0(b, y):
         bd, br = b // 8, b % 8
         for kd in range(8):
-            s_s[pl.ds(br * 8 * BS + (bd % 2) * 32 + kd * 4 + bd // 2, 8, stride=BS), :] = y[8 * kd:8 * (kd + 1)]
+            s_s[pl.ds(br * 8 * BS + (bd % 2) * 32 + kd * 4 + bd // 2, 8, stride=BS), :] = y[8 * kd : 8 * (kd + 1)]
+
     ket(0, put0)
 
-    def turn(i, _):
-        br, kr = i // 8, i % 8
-        z = s_s[pl.ds(pl.multiple_of(i * BS, 8), 64), :].T
-        z = jnp.concatenate([z[:64], z[64:]], axis=1)
+    def turned(i):
+        return jnp.concatenate([s_s[pl.ds(2 * i * BS, 64), :], s_s[pl.ds((2 * i + 1) * BS, 64), :]], axis=0).T
+
+    def turn(i):
+        br, kr = i // 4, 2 * (i % 4)
+        z = turned(i)
         for k1 in range(8):
-            x_s[pl.ds(pl.multiple_of((kr * 8 + k1) * 64 + br * 8, 8), 8), :] = z[8 * k1:8 * (k1 + 1)]
-        return 0
-    lax.fori_loop(0, 64, turn, 0)
-
-    bra(1)
+            z0, z1 = swap(z[8 * k1 : 8 * k1 + 8], z[64 + 8 * k1 : 64 + 8 * k1 + 8], low)
+            x_s[pl.ds(pl.multiple_of((kr * 8 + k1) * 64 + br * 8, 8), 8), :] = z0
+            x_s[pl.ds(pl.multiple_of((kr * 8 + 8 + k1) * 64 + br * 8, 8), 8), :] = z1
+
+    loop(32, UT, turn)
+    bra(1, second)
 
     def put1(b, y):
         bd, br = b // 8, b % 8
         for kd in range(8):
-            s_s[pl.ds(br * BS + kd * 8 + bd, 8, stride=8 * BS), :] = y[8 * kd:8 * (kd + 1)]
+            s_s[pl.ds(kd * 8 + bd + br * 8 * BS, 8, stride=BS), :] = y[8 * kd : 8 * (kd + 1)]
+
     ket(1, put1)
 
-    def leave(i, _):
-        z = s_s[pl.ds(pl.multiple_of(i * BS, 8), 64), :].T
+    def leave(i):
+        br, kr = i // 4, 2 * (i % 4)
+        z = turned(i)
         for e in range(2):
-            z_e = jnp.concatenate([z[64 * e:64 * e + 32], z[64 * e + 32:64 * e + 64]], axis=1)
-            for h in range(2):
-                out[2 * i + h, 16 * e:16 * (e + 1), :] = z_e[16 * h:16 * (h + 1)]
-        return 0
-    lax.fori_loop(0, 64, leave, 0)
+            for r in range(4):
+                z0, z1 = swap(z[64 * e + 8 * r : 64 * e + 8 * r + 8], z[64 * e + 32 + 8 * r : 64 * e + 40 + 8 * r], low)
+                h, row = r // 2, 16 * e + 8 * (r % 2)
+                out[2 * (kr * 8 + br) + h, row : row + 8, :] = z0
+                out[2 * (kr * 8 + 8 + br) + h, row : row + 8, :] = z1
+
+    loop(32, UT, leave)
+
 
 def absorb(env, p, ops):
     vm = pl.BlockSpec(memory_space=pltpu.VMEM)

time: 104 us -> 77.2 us (0.74)
  Pallas kernels: 43.4 us -> 17 us
    pallas_call x1, Pallas kernels: 36.9 us -> 10.5 us  [absorb(): pl.pallas_call(absorb_kernel, out_shape=jax.ShapeDtypeStruct((128, 32, 12...]
where the time goes in v1:
time: 77.2 us; the launch traced here: 76.9 us
  blocking collectives  55.5 us (72%)
  Pallas kernels  17 us (22%)
  local copies, waits for them, and re-layouts  3.8 us (5%)
    all_to_all x1, blocking collectives, body(): merged = lax.all_to_all(blocks, BITS, 0, 0, tiled=True)  41.7 us
    all_to_all x1, blocking collectives, body(): sums = lax.all_to_all(sums, BITS, 0, 0, tiled=True)  13.7 us
    pallas_call x1, Pallas kernels, absorb(): pl.pallas_call(absorb_kernel, out_shape=jax.ShapeDtypeStruct((128, 32, 12...  10.5 us
    pallas_call x1, Pallas kernels, scale(): pl.pallas_call(functools.partial(scale_kernel, entries), grid=(8,), out_s...  4.54 us
    unnamed x6, local copies, waits for them, and re-layouts  2.27 us
    pallas_call x1, Pallas kernels, gauge(): pl.pallas_call(gauge_kernel, out_shape=(jax.ShapeDtypeStruct((2, 128, 204...  1.96 us

profile of v1, /device:TPU:1, one launch (start us, length us, event | category | flops | bytes accessed | tf_op | source)
XLA Modules:
  0.0 76.9 jit_solution(7635243006458682703)
XLA Ops:
  0.6 1.5 %reshape.12.p = f32[256,64]{1,0:T(8,128)S(1)} reshape(f32[2,2,8,8,8,8]{5,4,3,2,1,0:T(8,128)} %param.5) | data formatting | bytes 131072 | tf_op jit(solution)/shard_map/reshape | solution.py:212
  2.2 0.0 copy-start.1
  2.2 1.6 %copy-done.1 = f32[2,1,64,4096]{3,2,1,0:T(8,128)S(1)} copy-done((f32[2,1,64,4096]{3,2,1,0:T(8,128)S(1)}, f32[2,1,64,4096]{3,2,1,0:T(8,128)}, u32[]{:S(2)}) %copy-start.1) | copy-done | bytes 2097176
  3.8 0.0 copy-start.2
  3.8 0.7 copy-done.2
  4.4 10.5 %absorb.1 = f32[128,32,128]{2,1,0:T(8,128)S(1)} custom-call(f32[2,1,64,4096]{3,2,1,0:T(8,128)S(1)} %copy-done.1, f32[256,64]{1,0:T(8,128)S(1)} %reshape.12.p, f32[2,2,2]{2,1,0:T(2,128)S(1)} %copy-done.2), custom_call_target="tpu_custom_call" | custom-call | flops 2147483648 | bytes 4194304 | tf_op jit(solution)/shard_map/absorb/pallas_call | solution.py:139
  14.9 0.0 copy-start
  14.9 41.7 %all_to_all.10 = f32[128,32,128]{2,1,0:T(8,128)S(1)} all-to-all(f32[128,32,128]{2,1,0:T(8,128)S(1)} %absorb.1), channel_id=1, replica_groups=mesh['bits_0'=4,'bits_1'=4,'bits_2'=4,'bits_3'=2] {'bits_0','bits_1','bi..., dimensions={0} | all-to-all | bytes 4194304 | tf_op jit(solution)/shard_map/all_to_all | solution.py:213
  56.7 0.0 copy-done
  56.7 2.0 %gauge.1 = (f32[2,128,2048]{2,1,0:T(8,128)S(1)}, f32[128,1,128]{2,1,0:T(1,128)S(1)}) custom-call(f32[4096,128]{1,0:T(8,128)S(1)} %bitcast.3, f32[128,128]{1,0:T(8,128)S(1)} %copy-done), custom_call_target="tpu_custom_call" | custom-call | flops 536870912 | bytes 4194304 | tf_op jit(solution)/shard_map/gauge/pallas_call | solution.py:176
  58.6 13.7 %all_to_all.11.sums = f32[128,1,128]{2,1,0:T(1,128)S(1)} all-to-all(f32[128,1,128]{2,1,0:T(1,128)S(1)} %get-tuple-element.5), channel_id=1, replica_groups=mesh['bits_0'=4,'bits_1'=4,'bits_2'=4,'bits_3'=2] {'bits_0','bits_1','bi..., dimensions={0} | all-to-all | bytes 131072 | tf_op jit(solution)/shard_map/all_to_all | solution.py:215
  72.4 4.5 %scale.1 = (f32[2,128,2048]{2,1,0:T(8,128)}, f32[2]{0:T(128)}) custom-call(f32[2,128,2048]{2,1,0:T(8,128)S(1)} %get-tuple-element.4.x, f32[128,1,128]{2,1,0:T(1,128)S(1)} %all_to_all.11.sums), custom_call_target="tpu_custom_call" | custom-call | flops 524288 | bytes 4194304 | tf_op jit(solution)/shard_map/scale/pallas_call | solution.py:200
Async XLA Ops:
  2.2 1.6 %copy-start.1 = (f32[2,1,64,4096]{3,2,1,0:T(8,128)S(1)}, f32[2,1,64,4096]{3,2,1,0:T(8,128)}, u32[]{:S(2)}) copy-start(f32[2,1,64,4096]{3,2,1,0:T(8,128)} %env.1) | copy-start | bytes 6291460
  3.8 0.7 copy-start.2
  14.9 41.8 %copy-start = (f32[128,128]{1,0:T(8,128)S(1)}, f32[128,128]{1,0:T(8,128)}, u32[]{:S(2)}) copy-start(f32[128,128]{1,0:T(8,128)} %gm.1) | copy-start | bytes 196612

commit v2 on v1

v2 whole, which is shorter than its diff:
```python
import functools

import jax
import jax.numpy as jnp
from jax import lax
from jax.experimental import pallas as pl
from jax.experimental.pallas import tpu as pltpu
from jax.sharding import Mesh
from jax.sharding import PartitionSpec as P

BITS = ("bits_0", "bits_1", "bits_2", "bits_3")
EPS = 1e-06
F32, BF16 = jnp.float32, jnp.bfloat16
RS = 132
BS = 68
G = 4
UB0 = 4
UB = 8
UK = 8
UT = 32


def halves(x):
    hi = x.astype(BF16)
    return hi, (x - hi.astype(F32)).astype(BF16)


def tall(x):
    hi, lo = halves(x)
    return jnp.concatenate([hi, lo, hi], axis=0)


def mm(w, x):
    return jnp.dot(w, tall(x), preferred_element_type=F32)


def loop(count, unroll, step):
    def several(i, carry):
        for u in range(unroll):
            step(i * unroll + u)
        return carry

    if unroll == count:
        several(0, 0)
    else:
        lax.fori_loop(0, count // unroll, several, 0)


def rows_at(at, size):
    return pl.ds(at if isinstance(at, int) else pl.multiple_of(at, 8), size)


def swap(a, b, low):
    return jnp.where(low, a, pltpu.roll(b, 64, 1)), jnp.where(low, pltpu.roll(a, 64, 1), b)


def absorb_kernel(env, p, ops, out, env_s, p_s, ops_s, x_s, t_s, s_s, bra_w, ket_w, env_sem, p_sem, ops_sem):
    small = [pltpu.make_async_copy(p, p_s, p_sem), pltpu.make_async_copy(ops, ops_s, ops_sem)]
    for copy in small:
        copy.start()

    def chunk(kl):
        rows = pl.ds(8 * kl, 8)
        return pltpu.make_async_copy(env.at[:, :, rows, :], env_s.at[:, :, rows, :], env_sem.at[kl])

    for kl in range(8):
        chunk(kl).start()
    low = lax.broadcasted_iota(jnp.int32, (8, 128), 1) < 64
    for copy in small:
        copy.wait()
    turned_p = jnp.swapaxes(p_s[...], 0, 1)
    w = jnp.concatenate([turned_p[d].T for d in range(8)], axis=0)
    row = lax.broadcasted_iota(jnp.int32, (64, 64), 0)
    col = lax.broadcasted_iota(jnp.int32, (64, 64), 1)
    exchange = jnp.where(row == (col % 8) * 8 + col // 8, 1.0, 0.0).astype(BF16)
    for j in range(2):
        wj = w[:, 128 * j : 128 * (j + 1)]
        hi, lo = halves(wj)
        ket_w[j] = jnp.concatenate([hi, hi, lo], axis=1)
        for a in range(2):
            parts = halves(ops_s[j, a, 0] * wj[:, :64] + ops_s[j, a, 1] * wj[:, 64:])
            if j == 0:
                parts = [jnp.dot(part, exchange, preferred_element_type=F32).astype(BF16) for part in parts]
            hi, lo = parts
            bra_w[j, 64 * a : 64 * (a + 1), :] = jnp.concatenate([hi, hi, lo], axis=1)

    def first(kl, k0):
        rows = rows_at(8 * kl, 8)
        pieces = []
        for c in range(4):
            lanes = pl.ds(k0 * 512 + 128 * c, 128)
            pieces += swap(env_s[0, 0, rows, lanes], env_s[1, 0, rows, lanes], low)
        return jnp.concatenate(pieces, axis=0)

    def second(at):
        return x_s[rows_at(at * 64, 64), :]

    def bra_group(j, at, xs):
        y = mm(bra_w[j], jnp.concatenate(xs, axis=1))
        for g in range(G):
            for a in range(2):
                t_s[pl.ds(a * 64 + at + g, 64, stride=RS), :] = y[64 * a : 64 * (a + 1), 128 * g : 128 * (g + 1)]

    def first_group(i):
        for kl_off in range(2):
            chunk(2 * i + kl_off).wait()
        for kl_off in range(2):
            kl = 2 * i + kl_off
            for k0 in range(0, 8, G):
                bra_group(0, kl * 8 + k0, [first(kl, k0 + g) for g in range(G)])

    loop(4, UB0 // 4, first_group)

    def ket(j, put):
        def step(i):
            x = jnp.concatenate([t_s[pl.ds((i * G + g) * RS, 128), :] for g in range(G)], axis=1)
            y = mm(ket_w[j], x)
            for g in range(G):
                put(i * G + g, y[:, 128 * g : 128 * (g + 1)])

        loop(64 // G, UK, step)

    def put0(b, y):
        bd, br = b // 8, b % 8
        for kd in range(8):
            s_s[pl.ds(br * 8 * BS + (bd % 2) * 32 + kd * 4 + bd // 2, 8, stride=BS), :] = y[8 * kd : 8 * (kd + 1)]

    ket(0, put0)

    def turned(i):
        return jnp.concatenate([s_s[pl.ds(2 * i * BS, 64), :], s_s[pl.ds((2 * i + 1) * BS, 64), :]], axis=0).T

    def turn(i):
        br, kr = i // 4, 2 * (i % 4)
        z = turned(i)
        for k1 in range(8):
            z0, z1 = swap(z[8 * k1 : 8 * k1 + 8], z[64 + 8 * k1 : 64 + 8 * k1 + 8], low)
            x_s[rows_at((kr * 8 + k1) * 64 + br * 8, 8), :] = z0
            x_s[rows_at((kr * 8 + 8 + k1) * 64 + br * 8, 8), :] = z1

    loop(32, UT, turn)
    loop(64 // G, UB, lambda i: bra_group(1, i * G, [second(i * G + g) for g in range(G)]))

    def put1(b, y):
        bd, br = b // 8, b % 8
        for kd in range(8):
            s_s[pl.ds(kd * 8 + bd + br * 8 * BS, 8, stride=BS), :] = y[8 * kd : 8 * (kd + 1)]

    ket(1, put1)

    def leave(i):
        br, kr = i // 4, 2 * (i % 4)
        z = turned(i)
        for e in range(2):
            for r in range(4):
                z0, z1 = swap(z[64 * e + 8 * r : 64 * e + 8 * r + 8], z[64 * e + 32 + 8 * r : 64 * e + 40 + 8 * r], low)
                h, row = r // 2, 16 * e + 8 * (r % 2)
                out[2 * (kr * 8 + br) + h, row : row + 8, :] = z0
                out[2 * (kr * 8 + 8 + br) + h, row : row + 8, :] = z1

    loop(32, UT, leave)


HBM = pl.BlockSpec(memory_space=pltpu.HBM)
VMEM = pl.BlockSpec(memory_space=pltpu.VMEM)


def absorb(env, p, ops):
    return pl.pallas_call(
        absorb_kernel,
        out_shape=jax.ShapeDtypeStruct((128, 32, 128), F32),
        in_specs=[HBM, HBM, HBM],
        out_specs=VMEM,
        scratch_shapes=[
            pltpu.VMEM((2, 1, 64, 4096), F32),
            pltpu.VMEM((256, 8, 8), F32),
            pltpu.SMEM((2, 2, 2), F32),
            pltpu.VMEM((4096, 128), F32),
            pltpu.VMEM((64 * RS, 128), F32),
            pltpu.VMEM((64 * BS, 128), F32),
            pltpu.VMEM((2, 128, 192), BF16),
            pltpu.VMEM((2, 64, 384), BF16),
            pltpu.SemaphoreType.DMA((8,)),
            pltpu.SemaphoreType.DMA,
            pltpu.SemaphoreType.DMA,
        ],
        compiler_params=pltpu.CompilerParams(vmem_limit_bytes=40 << 20),
        cost_estimate=pl.CostEstimate(flops=2 << 30, bytes_accessed=4 << 20, transcendentals=0),
        name="absorb",
    )(env, p, ops)


def absorb_raw(env, peps, ops):
    return absorb(*[pltpu.with_memory_space_constraint(v, pltpu.HBM) for v in (env, peps.reshape(256, 8, 8), ops)])


def gauge_kernel(r, gm, out, sq, w_s):
    hi, lo = halves(gm[...])
    w_s[...] = jnp.concatenate([hi, hi, lo], axis=1)
    lane = lax.broadcasted_iota(jnp.int32, (1, 128), 1)
    row = jnp.zeros((1, 128), F32)
    w = w_s[...]
    for e in range(2):
        tot = jnp.zeros((8, 128), F32)
        for b in range(0, 16, 4):
            x = jnp.concatenate([r[pl.ds(e * 16 + b + g, 128, stride=32), :] for g in range(4)], axis=1)
            y = mm(w, x)
            out[e, :, 128 * b : 128 * (b + 4)] = y
            q = (y * y).reshape(16, 8, 512).sum(0)
            for g in range(4):
                tot = tot + q[:, 128 * g : 128 * (g + 1)]
        row = jnp.where(lane == e, jnp.sum(tot), row)
    sq[...] = jnp.broadcast_to(row[None], (128, 1, 128))


def gauge(r, gm):
    return pl.pallas_call(
        gauge_kernel,
        out_shape=(jax.ShapeDtypeStruct((2, 128, 2048), F32), jax.ShapeDtypeStruct((128, 1, 128), F32)),
        in_specs=[VMEM, VMEM],
        out_specs=(VMEM, VMEM),
        scratch_shapes=[pltpu.VMEM((128, 384), BF16)],
        compiler_params=pltpu.CompilerParams(vmem_limit_bytes=40 << 20),
        cost_estimate=pl.CostEstimate(flops=1 << 29, bytes_accessed=4 << 20, transcendentals=0),
        name="gauge",
    )(r.reshape(4096, 128), gm)


def scale_kernel(entries, x, sums, out, rms, y_s, sems):
    total = jnp.sum(sums[...], axis=0)
    lane = lax.broadcasted_iota(jnp.int32, (1, 128), 1)
    copies = []
    for e in range(2):
        mean = jnp.sum(jnp.where(lane == e, total, 0.0), axis=1, keepdims=True) / entries
        factor = lax.rsqrt(mean + EPS)
        for c in range(8):
            at = pl.ds(16 * c, 16)
            y_s[e, at, :] = x[e, at, :] * factor
            copy = pltpu.make_async_copy(y_s.at[e, at, :], out.at[e, at, :], sems.at[8 * e + c])
            copy.start()
            copies.append(copy)
        rms[e] = jnp.sqrt(mean)[0, 0]
    for copy in copies:
        copy.wait()


def scale(x, sums, entries):
    return pl.pallas_call(
        functools.partial(scale_kernel, entries),
        out_shape=(jax.ShapeDtypeStruct((2, 128, 2048), F32), jax.ShapeDtypeStruct((2,), F32)),
        in_specs=[VMEM, VMEM],
        out_specs=(HBM, pl.BlockSpec(memory_space=pltpu.SMEM)),
        scratch_shapes=[pltpu.VMEM((2, 128, 2048), F32), pltpu.SemaphoreType.DMA((16,))],
        compiler_params=pltpu.CompilerParams(vmem_limit_bytes=40 << 20),
        cost_estimate=pl.CostEstimate(flops=1 << 19, bytes_accessed=4 << 20, transcendentals=0),
        name="scale",
    )(x, sums)


def body(environment, peps, operators, gauge_matrix):
    blocks = absorb_raw(environment, peps, operators)
    merged = lax.all_to_all(blocks, BITS, 0, 0, tiled=True)
    gauged, sums = gauge(merged, gauge_matrix)
    sums = lax.all_to_all(sums, BITS, 0, 0, tiled=True)
    entries = gauged.shape[1] * gauged.shape[2] * lax.axis_size(BITS)
    return scale(gauged, sums, entries)


def solution(mesh):
    torus = Mesh(mesh.devices.reshape(4, 4, 4, 2), BITS)
    in_specs = (P(None, BITS, None, None), P(), P(), P())
    out_specs = (P(None, None, BITS), P())
    return jax.shard_map(body, mesh=torus, in_specs=in_specs, out_specs=out_specs, check_vma=False)
```

time: 77.2 us -> 70.8 us (0.917)
  local copies, waits for them, and re-layouts: 3.8 us -> 0.01 us
  Pallas kernels: 17 us -> 14.5 us
    pallas_call x1, Pallas kernels: 4.54 us -> 2.18 us  [scale(): pl.pallas_call(functools.partial(scale_kernel, entries), out_shape=(jax.S...]
    unnamed x6 -> x2, local copies, waits for them, and re-layouts: 2.27 us -> 0.01 us
    reshape x1 -> x0, local copies, waits for them, and re-layouts: 1.53 us -> none  [body(): blocks = absorb(environment, peps.reshape(256, 64), operators)]
where the time goes in v2:
time: 70.8 us; the launch traced here: 70.6 us
  blocking collectives  55.5 us (78%)
  Pallas kernels  14.5 us (20%)
    all_to_all x1, blocking collectives, body(): merged = lax.all_to_all(blocks, BITS, 0, 0, tiled=True)  41.8 us
    all_to_all x1, blocking collectives, body(): sums = lax.all_to_all(sums, BITS, 0, 0, tiled=True)  13.7 us
    pallas_call x1, Pallas kernels, absorb(): pl.pallas_call(absorb_kernel, out_shape=jax.ShapeDtypeStruct((128, 32, 12...  10.4 us
    pallas_call x1, Pallas kernels, scale(): pl.pallas_call(functools.partial(scale_kernel, entries), out_shape=(jax.S...  2.18 us
    pallas_call x1, Pallas kernels, gauge(): pl.pallas_call(gauge_kernel, out_shape=(jax.ShapeDtypeStruct((2, 128, 204...  1.96 us

profile of v2, /device:TPU:1, one launch (start us, length us, event | category | flops | bytes accessed | tf_op | source)
XLA Modules:
  0.0 70.6 jit_solution(14609806099223928861)
XLA Ops:
  0.6 10.4 %absorb.1 = f32[128,32,128]{2,1,0:T(8,128)S(1)} custom-call(f32[2,1,64,4096]{3,2,1,0:T(8,128)} %env.1, f32[256,8,8]{2,1,0:T(8,128)} %bitcast.3, f32[2,2,2]{2,1,0:T(2,128)} %ops.1), custom_call_target="tpu_custom_call" | custom-call | flops 2147483648 | bytes 4194304 | tf_op jit(solution)/shard_map/absorb/pallas_call | solution.py:169
  11.0 0.0 copy-start
  11.0 41.8 %all_to_all.10 = f32[128,32,128]{2,1,0:T(8,128)S(1)} all-to-all(f32[128,32,128]{2,1,0:T(8,128)S(1)} %absorb.1), channel_id=1, replica_groups=mesh['bits_0'=4,'bits_1'=4,'bits_2'=4,'bits_3'=2] {'bits_0','bits_1','bi..., dimensions={0} | all-to-all | bytes 4194304 | tf_op jit(solution)/shard_map/all_to_all | solution.py:262
  52.8 0.0 copy-done
  52.8 2.0 %gauge.1 = (f32[2,128,2048]{2,1,0:T(8,128)S(1)}, f32[128,1,128]{2,1,0:T(1,128)S(1)}) custom-call(f32[4096,128]{1,0:T(8,128)S(1)} %bitcast.2, f32[128,128]{1,0:T(8,128)S(1)} %copy-done), custom_call_target="tpu_custom_call" | custom-call | flops 536870912 | bytes 4194304 | tf_op jit(solution)/shard_map/gauge/pallas_call | solution.py:217
  54.7 13.7 %all_to_all.11.sums = f32[128,1,128]{2,1,0:T(1,128)S(1)} all-to-all(f32[128,1,128]{2,1,0:T(1,128)S(1)} %get-tuple-element.5), channel_id=1, replica_groups=mesh['bits_0'=4,'bits_1'=4,'bits_2'=4,'bits_3'=2] {'bits_0','bits_1','bi..., dimensions={0} | all-to-all | bytes 131072 | tf_op jit(solution)/shard_map/all_to_all | solution.py:264
  68.4 2.2 %scale.1 = (f32[2,128,2048]{2,1,0:T(8,128)}, f32[2]{0:T(128)}) custom-call(f32[2,128,2048]{2,1,0:T(8,128)S(1)} %get-tuple-element.4.x, f32[128,1,128]{2,1,0:T(1,128)S(1)} %all_to_all.11.sums), custom_call_target="tpu_custom_call" | custom-call | flops 524288 | bytes 4194304 | tf_op jit(solution)/shard_map/scale/pallas_call | solution.py:248
Async XLA Ops:
  11.0 41.8 %copy-start = (f32[128,128]{1,0:T(8,128)S(1)}, f32[128,128]{1,0:T(8,128)}, u32[]{:S(2)}) copy-start(f32[128,128]{1,0:T(8,128)} %gm.1) | copy-start | bytes 196612

commit v3 on v2

--- a/solution.py
+++ b/solution.py
@@ -14,10 +14,10 @@
 RS = 132
 BS = 68
 G = 4
-UB0 = 4
-UB = 8
-UK = 8
-UT = 32
+W0 = 8
+UB = 16
+UBR = 8
+KM = 1
 
 
 def halves(x):
@@ -54,7 +54,7 @@
     return jnp.where(low, a, pltpu.roll(b, 64, 1)), jnp.where(low, pltpu.roll(a, 64, 1), b)
 
 
-def absorb_kernel(env, p, ops, out, env_s, p_s, ops_s, x_s, t_s, s_s, bra_w, ket_w, env_sem, p_sem, ops_sem):
+def absorb_kernel(env, p, ops, out, env_s, p_s, q_s, ops_s, x_s, t_s, s_s, bra_w, ket_w, env_sem, p_sem, ops_sem):
     small = [pltpu.make_async_copy(p, p_s, p_sem), pltpu.make_async_copy(ops, ops_s, ops_sem)]
     for copy in small:
         copy.start()
@@ -68,15 +68,16 @@
     low = lax.broadcasted_iota(jnp.int32, (8, 128), 1) < 64
     for copy in small:
         copy.wait()
-    turned_p = jnp.swapaxes(p_s[...], 0, 1)
-    w = jnp.concatenate([turned_p[d].T for d in range(8)], axis=0)
+    for g in range(32):
+        q_s[:, 8 * g : 8 * g + 8, :] = jnp.swapaxes(p_s[8 * g : 8 * g + 8], 0, 1)
     row = lax.broadcasted_iota(jnp.int32, (64, 64), 0)
     col = lax.broadcasted_iota(jnp.int32, (64, 64), 1)
     exchange = jnp.where(row == (col % 8) * 8 + col // 8, 1.0, 0.0).astype(BF16)
     for j in range(2):
-        wj = w[:, 128 * j : 128 * (j + 1)]
+        wj = jnp.concatenate([q_s[d, 128 * j : 128 * (j + 1), :].T for d in range(8)], axis=0)
         hi, lo = halves(wj)
-        ket_w[j] = jnp.concatenate([hi, hi, lo], axis=1)
+        ket_w[j, :64] = jnp.concatenate([hi, hi], axis=1)
+        ket_w[j, 64:] = jnp.concatenate([lo, jnp.zeros_like(lo)], axis=1)
         for a in range(2):
             parts = halves(ops_s[j, a, 0] * wj[:, :64] + ops_s[j, a, 1] * wj[:, 64:])
             if j == 0:
@@ -101,34 +102,40 @@
             for a in range(2):
                 t_s[pl.ds(a * 64 + at + g, 64, stride=RS), :] = y[64 * a : 64 * (a + 1), 128 * g : 128 * (g + 1)]
 
-    def first_group(i):
-        for kl_off in range(2):
-            chunk(2 * i + kl_off).wait()
-        for kl_off in range(2):
-            kl = 2 * i + kl_off
+    for start in range(0, 8, W0):
+        for kl in range(start, start + W0):
+            chunk(kl).wait()
+        for kl in range(start, start + W0):
             for k0 in range(0, 8, G):
                 bra_group(0, kl * 8 + k0, [first(kl, k0 + g) for g in range(G)])
 
-    loop(4, UB0 // 4, first_group)
-
-    def ket(j, put):
-        def step(i):
-            x = jnp.concatenate([t_s[pl.ds((i * G + g) * RS, 128), :] for g in range(G)], axis=1)
-            y = mm(ket_w[j], x)
+    def ket(j, br, put):
+        for start in range(0, 8, G):
+            x = jnp.concatenate([t_s[pl.ds(((start + g) * 8 + br) * RS, 128), :] for g in range(G)], axis=1)
+            x = jnp.concatenate(halves(x), axis=0)
+            if KM:
+                y = jnp.dot(ket_w[j], x, preferred_element_type=F32)
+                y = y[:64] + y[64:]
+            else:
+                y = jnp.dot(ket_w[j, :64], x, preferred_element_type=F32) + jnp.dot(ket_w[j, 64:], x, preferred_element_type=F32)
             for g in range(G):
-                put(i * G + g, y[:, 128 * g : 128 * (g + 1)])
-
-        loop(64 // G, UK, step)
+                put((start + g) * 8 + br, y[:, 128 * g : 128 * (g + 1)])
 
     def put0(b, y):
         bd, br = b // 8, b % 8
         for kd in range(8):
             s_s[pl.ds(br * 8 * BS + (bd % 2) * 32 + kd * 4 + bd // 2, 8, stride=BS), :] = y[8 * kd : 8 * (kd + 1)]
 
-    ket(0, put0)
-
     def turned(i):
         return jnp.concatenate([s_s[pl.ds(2 * i * BS, 64), :], s_s[pl.ds((2 * i + 1) * BS, 64), :]], axis=0).T
+
+    def sweep(j, put, finish):
+        def step(br):
+            ket(j, br, put)
+            for i in range(4):
+                finish(br * 4 + i)
+
+        loop(8, UBR, step)
 
     def turn(i):
         br, kr = i // 4, 2 * (i % 4)
@@ -138,15 +145,13 @@
             x_s[rows_at((kr * 8 + k1) * 64 + br * 8, 8), :] = z0
             x_s[rows_at((kr * 8 + 8 + k1) * 64 + br * 8, 8), :] = z1
 
-    loop(32, UT, turn)
+    sweep(0, put0, turn)
     loop(64 // G, UB, lambda i: bra_group(1, i * G, [second(i * G + g) for g in range(G)]))
 
     def put1(b, y):
         bd, br = b // 8, b % 8
         for kd in range(8):
             s_s[pl.ds(kd * 8 + bd + br * 8 * BS, 8, stride=BS), :] = y[8 * kd : 8 * (kd + 1)]
-
-    ket(1, put1)
 
     def leave(i):
         br, kr = i // 4, 2 * (i % 4)
@@ -158,7 +163,7 @@
                 out[2 * (kr * 8 + br) + h, row : row + 8, :] = z0
                 out[2 * (kr * 8 + 8 + br) + h, row : row + 8, :] = z1
 
-    loop(32, UT, leave)
+    sweep(1, put1, leave)
 
 
 HBM = pl.BlockSpec(memory_space=pltpu.HBM)
@@ -174,12 +179,13 @@
         scratch_shapes=[
             pltpu.VMEM((2, 1, 64, 4096), F32),
             pltpu.VMEM((256, 8, 8), F32),
+            pltpu.VMEM((8, 256, 8), F32),
             pltpu.SMEM((2, 2, 2), F32),
             pltpu.VMEM((4096, 128), F32),
             pltpu.VMEM((64 * RS, 128), F32),
             pltpu.VMEM((64 * BS, 128), F32),
             pltpu.VMEM((2, 128, 192), BF16),
-            pltpu.VMEM((2, 64, 384), BF16),
+            pltpu.VMEM((2, 128, 256), BF16),
             pltpu.SemaphoreType.DMA((8,)),
             pltpu.SemaphoreType.DMA,
             pltpu.SemaphoreType.DMA,

time: 70.8 us -> 67.7 us (0.956)
  Pallas kernels: 14.5 us -> 11.4 us
    pallas_call x1, Pallas kernels: 10.4 us -> 7.25 us  [absorb(): pl.pallas_call(absorb_kernel, out_shape=jax.ShapeDtypeStruct((128, 32, 12...]
where the time goes in v3:
time: 67.7 us; the launch traced here: 67.5 us
  blocking collectives  55.5 us (82%)
  Pallas kernels  11.4 us (17%)
    all_to_all x1, blocking collectives, body(): merged = lax.all_to_all(blocks, BITS, 0, 0, tiled=True)  41.8 us
    all_to_all x1, blocking collectives, body(): sums = lax.all_to_all(sums, BITS, 0, 0, tiled=True)  13.7 us
    pallas_call x1, Pallas kernels, absorb(): pl.pallas_call(absorb_kernel, out_shape=jax.ShapeDtypeStruct((128, 32, 12...  7.25 us
    pallas_call x1, Pallas kernels, scale(): pl.pallas_call(functools.partial(scale_kernel, entries), out_shape=(jax.S...  2.18 us
    pallas_call x1, Pallas kernels, gauge(): pl.pallas_call(gauge_kernel, out_shape=(jax.ShapeDtypeStruct((2, 128, 204...  1.96 us

profile of v3, /device:TPU:1, one launch (start us, length us, event | category | flops | bytes accessed | tf_op | source)
XLA Modules:
  0.0 67.5 jit_solution(1318302850688011035)
XLA Ops:
  0.6 7.3 %absorb.1 = f32[128,32,128]{2,1,0:T(8,128)S(1)} custom-call(f32[2,1,64,4096]{3,2,1,0:T(8,128)} %env.1, f32[256,8,8]{2,1,0:T(8,128)} %bitcast.3, f32[2,2,2]{2,1,0:T(2,128)} %ops.1), custom_call_target="tpu_custom_call" | custom-call | flops 2147483648 | bytes 4194304 | tf_op jit(solution)/shard_map/absorb/pallas_call | solution.py:174
  7.9 0.0 copy-start
  7.9 41.8 %all_to_all.10 = f32[128,32,128]{2,1,0:T(8,128)S(1)} all-to-all(f32[128,32,128]{2,1,0:T(8,128)S(1)} %absorb.1), channel_id=1, replica_groups=mesh['bits_0'=4,'bits_1'=4,'bits_2'=4,'bits_3'=2] {'bits_0','bits_1','bi..., dimensions={0} | all-to-all | bytes 4194304 | tf_op jit(solution)/shard_map/all_to_all | solution.py:268
  49.7 0.0 copy-done
  49.7 2.0 %gauge.1 = (f32[2,128,2048]{2,1,0:T(8,128)S(1)}, f32[128,1,128]{2,1,0:T(1,128)S(1)}) custom-call(f32[4096,128]{1,0:T(8,128)S(1)} %bitcast.2, f32[128,128]{1,0:T(8,128)S(1)} %copy-done), custom_call_target="tpu_custom_call" | custom-call | flops 536870912 | bytes 4194304 | tf_op jit(solution)/shard_map/gauge/pallas_call | solution.py:223
  51.6 13.7 %all_to_all.11.sums = f32[128,1,128]{2,1,0:T(1,128)S(1)} all-to-all(f32[128,1,128]{2,1,0:T(1,128)S(1)} %get-tuple-element.5), channel_id=1, replica_groups=mesh['bits_0'=4,'bits_1'=4,'bits_2'=4,'bits_3'=2] {'bits_0','bits_1','bi..., dimensions={0} | all-to-all | bytes 131072 | tf_op jit(solution)/shard_map/all_to_all | solution.py:270
  65.3 2.2 %scale.1 = (f32[2,128,2048]{2,1,0:T(8,128)}, f32[2]{0:T(128)}) custom-call(f32[2,128,2048]{2,1,0:T(8,128)S(1)} %get-tuple-element.4.x, f32[128,1,128]{2,1,0:T(1,128)S(1)} %all_to_all.11.sums), custom_call_target="tpu_custom_call" | custom-call | flops 524288 | bytes 4194304 | tf_op jit(solution)/shard_map/scale/pallas_call | solution.py:254
Async XLA Ops:
  7.9 41.8 %copy-start = (f32[128,128]{1,0:T(8,128)S(1)}, f32[128,128]{1,0:T(8,128)}, u32[]{:S(2)}) copy-start(f32[128,128]{1,0:T(8,128)} %gm.1) | copy-start | bytes 196612

commit v4 on v3

--- a/solution.py
+++ b/solution.py
@@ -64,7 +64,7 @@
         return pltpu.make_async_copy(env.at[:, :, rows, :], env_s.at[:, :, rows, :], env_sem.at[kl])
 
     for kl in range(8):
-        chunk(kl).start()
+        chunk(kl).start(priority=1)
     low = lax.broadcasted_iota(jnp.int32, (8, 128), 1) < 64
     for copy in small:
         copy.wait()
@@ -200,52 +200,60 @@
     return absorb(*[pltpu.with_memory_space_constraint(v, pltpu.HBM) for v in (env, peps.reshape(256, 8, 8), ops)])
 
 
-def gauge_kernel(r, gm, out, sq, w_s):
+def gauge_kernel(r, gm, out, sq, w_s, x_s):
     hi, lo = halves(gm[...])
-    w_s[...] = jnp.concatenate([hi, hi, lo], axis=1)
-    lane = lax.broadcasted_iota(jnp.int32, (1, 128), 1)
-    row = jnp.zeros((1, 128), F32)
-    w = w_s[...]
+    w_s[:128] = jnp.concatenate([hi, hi], axis=1)
+    w_s[128:] = jnp.concatenate([lo, jnp.zeros_like(lo)], axis=1)
+    for t in range(4):
+        for m in range(16):
+            part = jnp.swapaxes(r[8 * m : 8 * m + 8, 8 * t : 8 * t + 8, :], 0, 1)
+            for s in range(8):
+                x_s[8 * t + s, 8 * m : 8 * m + 8, :] = part[s]
+    low = lax.broadcasted_iota(jnp.int32, (1, 128), 1) < 64
+    sums = []
     for e in range(2):
         tot = jnp.zeros((8, 128), F32)
         for b in range(0, 16, 4):
-            x = jnp.concatenate([r[pl.ds(e * 16 + b + g, 128, stride=32), :] for g in range(4)], axis=1)
-            y = mm(w, x)
+            x = jnp.concatenate([x_s[e * 16 + b + g] for g in range(4)], axis=1)
+            y = jnp.dot(w_s[...], jnp.concatenate(halves(x), axis=0), preferred_element_type=F32)
+            y = y[:128] + y[128:]
             out[e, :, 128 * b : 128 * (b + 4)] = y
             q = (y * y).reshape(16, 8, 512).sum(0)
             for g in range(4):
                 tot = tot + q[:, 128 * g : 128 * (g + 1)]
-        row = jnp.where(lane == e, jnp.sum(tot), row)
-    sq[...] = jnp.broadcast_to(row[None], (128, 1, 128))
+        sums.append(jnp.sum(tot))
+    sq[...] = jnp.broadcast_to(jnp.where(low, sums[0], sums[1]), (128, 128))
 
 
 def gauge(r, gm):
     return pl.pallas_call(
         gauge_kernel,
-        out_shape=(jax.ShapeDtypeStruct((2, 128, 2048), F32), jax.ShapeDtypeStruct((128, 1, 128), F32)),
+        out_shape=(jax.ShapeDtypeStruct((2, 128, 2048), F32), jax.ShapeDtypeStruct((128, 128), F32)),
         in_specs=[VMEM, VMEM],
         out_specs=(VMEM, VMEM),
-        scratch_shapes=[pltpu.VMEM((128, 384), BF16)],
+        scratch_shapes=[pltpu.VMEM((256, 256), BF16), pltpu.VMEM((32, 128, 128), F32)],
         compiler_params=pltpu.CompilerParams(vmem_limit_bytes=40 << 20),
         cost_estimate=pl.CostEstimate(flops=1 << 29, bytes_accessed=4 << 20, transcendentals=0),
         name="gauge",
-    )(r.reshape(4096, 128), gm)
+    )(r, gm)
 
 
 def scale_kernel(entries, x, sums, out, rms, y_s, sems):
-    total = jnp.sum(sums[...], axis=0)
-    lane = lax.broadcasted_iota(jnp.int32, (1, 128), 1)
+    total = jnp.sum(sums[...], axis=0, keepdims=True)
+    low = lax.broadcasted_iota(jnp.int32, (1, 128), 1) < 64
+    other = pltpu.roll(total, 64, 1)
     copies = []
+    means = [jnp.where(low, total, other) / entries, jnp.where(low, other, total) / entries]
     for e in range(2):
-        mean = jnp.sum(jnp.where(lane == e, total, 0.0), axis=1, keepdims=True) / entries
-        factor = lax.rsqrt(mean + EPS)
-        for c in range(8):
-            at = pl.ds(16 * c, 16)
+        factor = jnp.concatenate([lax.rsqrt(means[e] + EPS)] * 16, axis=1)
+        for c in range(4):
+            at = pl.ds(128 // 4 * c, 128 // 4)
             y_s[e, at, :] = x[e, at, :] * factor
-            copy = pltpu.make_async_copy(y_s.at[e, at, :], out.at[e, at, :], sems.at[8 * e + c])
+            copy = pltpu.make_async_copy(y_s.at[e, at, :], out.at[e, at, :], sems.at[4 * e + c])
             copy.start()
             copies.append(copy)
-        rms[e] = jnp.sqrt(mean)[0, 0]
+    for e in range(2):
+        rms[e] = jnp.sqrt(means[e])[0, 0]
     for copy in copies:
         copy.wait()
 
@@ -256,7 +264,7 @@
         out_shape=(jax.ShapeDtypeStruct((2, 128, 2048), F32), jax.ShapeDtypeStruct((2,), F32)),
         in_specs=[VMEM, VMEM],
         out_specs=(HBM, pl.BlockSpec(memory_space=pltpu.SMEM)),
-        scratch_shapes=[pltpu.VMEM((2, 128, 2048), F32), pltpu.SemaphoreType.DMA((16,))],
+        scratch_shapes=[pltpu.VMEM((2, 128, 2048), F32), pltpu.SemaphoreType.DMA((2 * 4,))],
         compiler_params=pltpu.CompilerParams(vmem_limit_bytes=40 << 20),
         cost_estimate=pl.CostEstimate(flops=1 << 19, bytes_accessed=4 << 20, transcendentals=0),
         name="scale",

time: 67.7 us -> 66.4 us (0.981)
  Pallas kernels: 11.4 us -> 10 us
    pallas_call x1, Pallas kernels: 1.96 us -> 1.19 us  [gauge(): pl.pallas_call(gauge_kernel, out_shape=(jax.ShapeDtypeStruct((2, 128, 204...]
where the time goes in v4:
time: 66.4 us; the launch traced here: 66.2 us
  blocking collectives  55.5 us (84%)
  Pallas kernels  10 us (15%)
    all_to_all x1, blocking collectives, body(): merged = lax.all_to_all(blocks, BITS, 0, 0, tiled=True)  41.7 us
    all_to_all x1, blocking collectives, body(): sums = lax.all_to_all(sums, BITS, 0, 0, tiled=True)  13.7 us
    pallas_call x1, Pallas kernels, absorb(): pl.pallas_call(absorb_kernel, out_shape=jax.ShapeDtypeStruct((128, 32, 12...  6.84 us
    pallas_call x1, Pallas kernels, scale(): pl.pallas_call(functools.partial(scale_kernel, entries), out_shape=(jax.S...  2.01 us

profile of v4, /device:TPU:1, one launch (start us, length us, event | category | flops | bytes accessed | tf_op | source)
XLA Modules:
  0.0 66.2 jit_solution(1986732973028079454)
XLA Ops:
  0.6 6.8 %absorb.1 = f32[128,32,128]{2,1,0:T(8,128)S(1)} custom-call(f32[2,1,64,4096]{3,2,1,0:T(8,128)} %env.1, f32[256,8,8]{2,1,0:T(8,128)} %bitcast.7, f32[2,2,2]{2,1,0:T(2,128)} %ops.1), custom_call_target="tpu_custom_call" | custom-call | flops 2147483648 | bytes 4194304 | tf_op jit(solution)/shard_map/absorb/pallas_call | solution.py:174
  7.5 0.0 copy-start
  7.5 41.7 %all_to_all.16.r = f32[128,32,128]{2,1,0:T(8,128)S(1)} all-to-all(f32[128,32,128]{2,1,0:T(8,128)S(1)} %absorb.1), channel_id=1, replica_groups=mesh['bits_0'=4,'bits_1'=4,'bits_2'=4,'bits_3'=2] {'bits_0','bits_1','bi..., dimensions={0} | all-to-all | bytes 4194304 | tf_op jit(solution)/shard_map/all_to_all | solution.py:276
  49.2 0.0 copy-done
  49.2 1.2 %gauge.1 = (f32[2,128,2048]{2,1,0:T(8,128)S(1)}, f32[128,128]{1,0:T(8,128)S(1)}) custom-call(f32[128,32,128]{2,1,0:T(8,128)S(1)} %all_to_all.16.r, f32[128,128]{1,0:T(8,128)S(1)} %copy-done), custom_call_target="tpu_custom_call" | custom-call | flops 536870912 | bytes 4194304 | tf_op jit(solution)/shard_map/gauge/pallas_call | solution.py:229
  50.4 13.7 %all_to_all.17 = f32[128,1,128]{2,1,0:T(1,128)S(1)} all-to-all(f32[128,1,128]{2,1,0:T(1,128)S(1)} %bitcast.6), channel_id=1, replica_groups=mesh['bits_0'=4,'bits_1'=4,'bits_2'=4,'bits_3'=2] {'bits_0','bits_1','bi..., dimensions={0} | all-to-all | bytes 131072 | tf_op jit(solution)/shard_map/all_to_all | solution.py:278
  64.2 2.0 %scale.1 = (f32[2,128,2048]{2,1,0:T(8,128)}, f32[2]{0:T(128)}) custom-call(f32[2,128,2048]{2,1,0:T(8,128)S(1)} %get-tuple-element.4.x, f32[128,128]{1,0:T(8,128)S(1)} %bitcast.5), custom_call_target="tpu_custom_call" | custom-call | flops 524288 | bytes 4194304 | tf_op jit(solution)/shard_map/scale/pallas_call | solution.py:262
Async XLA Ops:
  7.5 41.8 %copy-start = (f32[128,128]{1,0:T(8,128)S(1)}, f32[128,128]{1,0:T(8,128)}, u32[]{:S(2)}) copy-start(f32[128,128]{1,0:T(8,128)} %gm.1) | copy-start | bytes 196612

commit v5 on v4

--- a/solution.py
+++ b/solution.py
@@ -18,6 +18,7 @@
 UB = 16
 UBR = 8
 KM = 1
+LATE = 1
 
 
 def halves(x):
@@ -68,22 +69,21 @@
     low = lax.broadcasted_iota(jnp.int32, (8, 128), 1) < 64
     for copy in small:
         copy.wait()
-    for g in range(32):
-        q_s[:, 8 * g : 8 * g + 8, :] = jnp.swapaxes(p_s[8 * g : 8 * g + 8], 0, 1)
-    row = lax.broadcasted_iota(jnp.int32, (64, 64), 0)
-    col = lax.broadcasted_iota(jnp.int32, (64, 64), 1)
-    exchange = jnp.where(row == (col % 8) * 8 + col // 8, 1.0, 0.0).astype(BF16)
-    for j in range(2):
-        wj = jnp.concatenate([q_s[d, 128 * j : 128 * (j + 1), :].T for d in range(8)], axis=0)
-        hi, lo = halves(wj)
+    def weights(j):
+        for g in range(16):
+            part = pl.ds(64 * (g // 8) + g % 8, 8, stride=8) if j == 0 else pl.ds(128 + 8 * g, 8)
+            q_s[:, 128 * j + 8 * g : 128 * j + 8 * g + 8, :] = jnp.swapaxes(p_s[part], 0, 1)
+        w = jnp.concatenate([q_s[d, 128 * j : 128 * (j + 1), :].T for d in range(8)], axis=0)
+        for a in range(2):
+            hi, lo = halves(ops_s[j, a, 0] * w[:, :64] + ops_s[j, a, 1] * w[:, 64:])
+            bra_w[j, 64 * a : 64 * (a + 1), :] = jnp.concatenate([hi, hi, lo], axis=1)
+        hi, lo = halves(w)
         ket_w[j, :64] = jnp.concatenate([hi, hi], axis=1)
         ket_w[j, 64:] = jnp.concatenate([lo, jnp.zeros_like(lo)], axis=1)
-        for a in range(2):
-            parts = halves(ops_s[j, a, 0] * wj[:, :64] + ops_s[j, a, 1] * wj[:, 64:])
-            if j == 0:
-                parts = [jnp.dot(part, exchange, preferred_element_type=F32).astype(BF16) for part in parts]
-            hi, lo = parts
-            bra_w[j, 64 * a : 64 * (a + 1), :] = jnp.concatenate([hi, hi, lo], axis=1)
+
+    weights(0)
+    if not LATE:
+        weights(1)
 
     def first(kl, k0):
         rows = rows_at(8 * kl, 8)
@@ -96,18 +96,18 @@
     def second(at):
         return x_s[rows_at(at * 64, 64), :]
 
-    def bra_group(j, at, xs):
+    def bra_group(j, places, xs):
         y = mm(bra_w[j], jnp.concatenate(xs, axis=1))
         for g in range(G):
             for a in range(2):
-                t_s[pl.ds(a * 64 + at + g, 64, stride=RS), :] = y[64 * a : 64 * (a + 1), 128 * g : 128 * (g + 1)]
+                t_s[pl.ds(a * 64 + places[g], 64, stride=RS), :] = y[64 * a : 64 * (a + 1), 128 * g : 128 * (g + 1)]
 
     for start in range(0, 8, W0):
         for kl in range(start, start + W0):
             chunk(kl).wait()
         for kl in range(start, start + W0):
             for k0 in range(0, 8, G):
-                bra_group(0, kl * 8 + k0, [first(kl, k0 + g) for g in range(G)])
+                bra_group(0, [(k0 + g) * 8 + kl for g in range(G)], [first(kl, k0 + g) for g in range(G)])
 
     def ket(j, br, put):
         for start in range(0, 8, G):
@@ -145,8 +145,10 @@
             x_s[rows_at((kr * 8 + k1) * 64 + br * 8, 8), :] = z0
             x_s[rows_at((kr * 8 + 8 + k1) * 64 + br * 8, 8), :] = z1
 
+    if LATE:
+        weights(1)
     sweep(0, put0, turn)
-    loop(64 // G, UB, lambda i: bra_group(1, i * G, [second(i * G + g) for g in range(G)]))
+    loop(64 // G, UB, lambda i: bra_group(1, [i * G + g for g in range(G)], [second(i * G + g) for g in range(G)]))
 
     def put1(b, y):
         bd, br = b // 8, b % 8
@@ -238,7 +240,7 @@
     )(r, gm)
 
 
-def scale_kernel(entries, x, sums, out, rms, y_s, sems):
+def scale_kernel(entries, x, sums, out, rms, y_s, rms_s, sems, rms_sem):
     total = jnp.sum(sums[...], axis=0, keepdims=True)
     low = lax.broadcasted_iota(jnp.int32, (1, 128), 1) < 64
     other = pltpu.roll(total, 64, 1)
@@ -253,7 +255,10 @@
             copy.start()
             copies.append(copy)
     for e in range(2):
-        rms[e] = jnp.sqrt(means[e])[0, 0]
+        rms_s[e] = jnp.sqrt(means[e])[0, 0]
+    copy = pltpu.make_async_copy(rms_s, rms, rms_sem)
+    copy.start()
+    copies.append(copy)
     for copy in copies:
         copy.wait()
 
@@ -263,8 +268,13 @@
         functools.partial(scale_kernel, entries),
         out_shape=(jax.ShapeDtypeStruct((2, 128, 2048), F32), jax.ShapeDtypeStruct((2,), F32)),
         in_specs=[VMEM, VMEM],
-        out_specs=(HBM, pl.BlockSpec(memory_space=pltpu.SMEM)),
-        scratch_shapes=[pltpu.VMEM((2, 128, 2048), F32), pltpu.SemaphoreType.DMA((2 * 4,))],
+        out_specs=(HBM, HBM),
+        scratch_shapes=[
+            pltpu.VMEM((2, 128, 2048), F32),
+            pltpu.SMEM((2,), F32),
+            pltpu.SemaphoreType.DMA((2 * 4,)),
+            pltpu.SemaphoreType.DMA,
+        ],
         compiler_params=pltpu.CompilerParams(vmem_limit_bytes=40 << 20),
         cost_estimate=pl.CostEstimate(flops=1 << 19, bytes_accessed=4 << 20, transcendentals=0),
         name="scale",

time: 66.4 us -> 65.9 us (level)
  no operation moved by 1% of the time
where the time goes in v5:
time: 65.9 us; the launch traced here: 65.7 us
  blocking collectives  55.5 us (84%)
  Pallas kernels  9.52 us (14%)
  between operations  0.66 us (1%)
    all_to_all x1, blocking collectives, body(): merged = lax.all_to_all(blocks, BITS, 0, 0, tiled=True)  41.8 us
    all_to_all x1, blocking collectives, body(): sums = lax.all_to_all(sums, BITS, 0, 0, tiled=True)  13.7 us
    pallas_call x1, Pallas kernels, absorb(): pl.pallas_call(absorb_kernel, out_shape=jax.ShapeDtypeStruct((128, 32, 12...  6.81 us
    pallas_call x1, Pallas kernels, scale(): pl.pallas_call(functools.partial(scale_kernel, entries), out_shape=(jax.S...  1.51 us

profile of v5, /device:TPU:1, one launch (start us, length us, event | category | flops | bytes accessed | tf_op | source)
XLA Modules:
  0.0 65.7 jit_solution(16112860201933289985)
XLA Ops:
  0.6 6.8 %absorb.1 = f32[128,32,128]{2,1,0:T(8,128)S(1)} custom-call(f32[2,1,64,4096]{3,2,1,0:T(8,128)} %env.1, f32[256,8,8]{2,1,0:T(8,128)} %bitcast.7, f32[2,2,2]{2,1,0:T(2,128)} %ops.1), custom_call_target="tpu_custom_call" | custom-call | flops 2147483648 | bytes 4194304 | tf_op jit(solution)/shard_map/absorb/pallas_call | solution.py:176
  7.4 0.0 copy-start
  7.5 41.8 %all_to_all.16.r = f32[128,32,128]{2,1,0:T(8,128)S(1)} all-to-all(f32[128,32,128]{2,1,0:T(8,128)S(1)} %absorb.1), channel_id=1, replica_groups=mesh['bits_0'=4,'bits_1'=4,'bits_2'=4,'bits_3'=2] {'bits_0','bits_1','bi..., dimensions={0} | all-to-all | bytes 4194304 | tf_op jit(solution)/shard_map/all_to_all | solution.py:286
  49.2 0.0 copy-done
  49.2 1.2 %gauge.1 = (f32[2,128,2048]{2,1,0:T(8,128)S(1)}, f32[128,128]{1,0:T(8,128)S(1)}) custom-call(f32[128,32,128]{2,1,0:T(8,128)S(1)} %all_to_all.16.r, f32[128,128]{1,0:T(8,128)S(1)} %copy-done), custom_call_target="tpu_custom_call" | custom-call | flops 536870912 | bytes 4194304 | tf_op jit(solution)/shard_map/gauge/pallas_call | solution.py:231
  50.4 13.7 %all_to_all.17 = f32[128,1,128]{2,1,0:T(1,128)S(1)} all-to-all(f32[128,1,128]{2,1,0:T(1,128)S(1)} %bitcast.6), channel_id=1, replica_groups=mesh['bits_0'=4,'bits_1'=4,'bits_2'=4,'bits_3'=2] {'bits_0','bits_1','bi..., dimensions={0} | all-to-all | bytes 131072 | tf_op jit(solution)/shard_map/all_to_all | solution.py:288
  64.2 1.5 %scale.1 = (f32[2,128,2048]{2,1,0:T(8,128)}, f32[2]{0:T(128)}) custom-call(f32[2,128,2048]{2,1,0:T(8,128)S(1)} %get-tuple-element.4.x, f32[128,128]{1,0:T(8,128)S(1)} %bitcast.5), custom_call_target="tpu_custom_call" | custom-call | flops 524288 | bytes 4194304 | tf_op jit(solution)/shard_map/scale/pallas_call | solution.py:267
Async XLA Ops:
  7.4 41.8 %copy-start = (f32[128,128]{1,0:T(8,128)S(1)}, f32[128,128]{1,0:T(8,128)}, u32[]{:S(2)}) copy-start(f32[128,128]{1,0:T(8,128)} %gm.1) | copy-start | bytes 196612

commit v6 on v5

--- a/solution.py
+++ b/solution.py
@@ -206,24 +206,25 @@
     hi, lo = halves(gm[...])
     w_s[:128] = jnp.concatenate([hi, hi], axis=1)
     w_s[128:] = jnp.concatenate([lo, jnp.zeros_like(lo)], axis=1)
-    for t in range(4):
-        for m in range(16):
-            part = jnp.swapaxes(r[8 * m : 8 * m + 8, 8 * t : 8 * t + 8, :], 0, 1)
-            for s in range(8):
-                x_s[8 * t + s, 8 * m : 8 * m + 8, :] = part[s]
     low = lax.broadcasted_iota(jnp.int32, (1, 128), 1) < 64
     sums = []
     for e in range(2):
         tot = jnp.zeros((8, 128), F32)
-        for b in range(0, 16, 4):
-            x = jnp.concatenate([x_s[e * 16 + b + g] for g in range(4)], axis=1)
-            y = jnp.dot(w_s[...], jnp.concatenate(halves(x), axis=0), preferred_element_type=F32)
-            y = y[:128] + y[128:]
-            out[e, :, 128 * b : 128 * (b + 4)] = y
-            q = (y * y).reshape(16, 8, 512).sum(0)
-            for g in range(4):
-                tot = tot + q[:, 128 * g : 128 * (g + 1)]
-        sums.append(jnp.sum(tot))
+        for t in (2 * e, 2 * e + 1):
+            for m in range(16):
+                part = jnp.swapaxes(r[8 * m : 8 * m + 8, 8 * t : 8 * t + 8, :], 0, 1)
+                for s in range(8):
+                    x_s[8 * t + s, 8 * m : 8 * m + 8, :] = part[s]
+            for b in range(8 * t, 8 * t + 8, 4):
+                x = jnp.concatenate([x_s[b + g] for g in range(4)], axis=1)
+                y = jnp.dot(w_s[...], jnp.concatenate(halves(x), axis=0), preferred_element_type=F32)
+                y = y[:128] + y[128:]
+                out[e, :, 128 * (b - 16 * e) : 128 * (b - 16 * e + 4)] = y
+                q = (y * y).reshape(16, 8, 128 * 4).sum(0)
+                for g in range(4):
+                    tot = tot + q[:, 128 * g : 128 * (g + 1)]
+        part = jnp.sum(tot, axis=0, keepdims=True)
+        sums.append(part + pltpu.roll(part, 64, 1))
     sq[...] = jnp.broadcast_to(jnp.where(low, sums[0], sums[1]), (128, 128))
 
 
@@ -243,11 +244,10 @@
 def scale_kernel(entries, x, sums, out, rms, y_s, rms_s, sems, rms_sem):
     total = jnp.sum(sums[...], axis=0, keepdims=True)
     low = lax.broadcasted_iota(jnp.int32, (1, 128), 1) < 64
-    other = pltpu.roll(total, 64, 1)
     copies = []
-    means = [jnp.where(low, total, other) / entries, jnp.where(low, other, total) / entries]
+    means = [jnp.sum(jnp.where(half, total, 0.0), axis=1, keepdims=True) / entries for half in (low, ~low)]
     for e in range(2):
-        factor = jnp.concatenate([lax.rsqrt(means[e] + EPS)] * 16, axis=1)
+        factor = lax.rsqrt(means[e] + EPS)
         for c in range(4):
             at = pl.ds(128 // 4 * c, 128 // 4)
             y_s[e, at, :] = x[e, at, :] * factor

time: 65.9 us -> 65.8 us (level)
  no operation moved by 1% of the time
where the time goes in v6:
time: 65.8 us; the launch traced here: 65.6 us
  blocking collectives  55.5 us (84%)
  Pallas kernels  9.48 us (14%)
    all_to_all x1, blocking collectives, body(): merged = lax.all_to_all(blocks, BITS, 0, 0, tiled=True)  41.8 us
    all_to_all x1, blocking collectives, body(): sums = lax.all_to_all(sums, BITS, 0, 0, tiled=True)  13.7 us
    pallas_call x1, Pallas kernels, absorb(): pl.pallas_call(absorb_kernel, out_shape=jax.ShapeDtypeStruct((128, 32, 12...  6.81 us
    pallas_call x1, Pallas kernels, scale(): pl.pallas_call(functools.partial(scale_kernel, entries), out_shape=(jax.S...  1.52 us

profile of v6, /device:TPU:1, one launch (start us, length us, event | category | flops | bytes accessed | tf_op | source)
XLA Modules:
  0.0 65.6 jit_solution(2577672855275578447)
XLA Ops:
  0.6 6.8 %absorb.1 = f32[128,32,128]{2,1,0:T(8,128)S(1)} custom-call(f32[2,1,64,4096]{3,2,1,0:T(8,128)} %env.1, f32[256,8,8]{2,1,0:T(8,128)} %bitcast.7, f32[2,2,2]{2,1,0:T(2,128)} %ops.1), custom_call_target="tpu_custom_call" | custom-call | flops 2147483648 | bytes 4194304 | tf_op jit(solution)/shard_map/absorb/pallas_call | solution.py:176
  7.4 0.0 copy-start
  7.5 41.8 %all_to_all.16.r = f32[128,32,128]{2,1,0:T(8,128)S(1)} all-to-all(f32[128,32,128]{2,1,0:T(8,128)S(1)} %absorb.1), channel_id=1, replica_groups=mesh['bits_0'=4,'bits_1'=4,'bits_2'=4,'bits_3'=2] {'bits_0','bits_1','bi..., dimensions={0} | all-to-all | bytes 4194304 | tf_op jit(solution)/shard_map/all_to_all | solution.py:286
  49.2 0.0 copy-done
  49.2 1.2 %gauge.1 = (f32[2,128,2048]{2,1,0:T(8,128)S(1)}, f32[128,128]{1,0:T(8,128)S(1)}) custom-call(f32[128,32,128]{2,1,0:T(8,128)S(1)} %all_to_all.16.r, f32[128,128]{1,0:T(8,128)S(1)} %copy-done), custom_call_target="tpu_custom_call" | custom-call | flops 536870912 | bytes 4194304 | tf_op jit(solution)/shard_map/gauge/pallas_call | solution.py:232
  50.4 13.7 %all_to_all.17 = f32[128,1,128]{2,1,0:T(1,128)S(1)} all-to-all(f32[128,1,128]{2,1,0:T(1,128)S(1)} %bitcast.6), channel_id=1, replica_groups=mesh['bits_0'=4,'bits_1'=4,'bits_2'=4,'bits_3'=2] {'bits_0','bits_1','bi..., dimensions={0} | all-to-all | bytes 131072 | tf_op jit(solution)/shard_map/all_to_all | solution.py:288
  64.1 1.5 %scale.1 = (f32[2,128,2048]{2,1,0:T(8,128)}, f32[2]{0:T(128)}) custom-call(f32[2,128,2048]{2,1,0:T(8,128)S(1)} %get-tuple-element.4.x, f32[128,128]{1,0:T(8,128)S(1)} %bitcast.5), custom_call_target="tpu_custom_call" | custom-call | flops 524288 | bytes 4194304 | tf_op jit(solution)/shard_map/scale/pallas_call | solution.py:267
Async XLA Ops:
  7.4 41.8 %copy-start = (f32[128,128]{1,0:T(8,128)S(1)}, f32[128,128]{1,0:T(8,128)}, u32[]{:S(2)}) copy-start(f32[128,128]{1,0:T(8,128)} %gm.1) | copy-start | bytes 196612

commit v7 on v6

--- a/solution.py
+++ b/solution.py
@@ -56,7 +56,11 @@
 
 
 def absorb_kernel(env, p, ops, out, env_s, p_s, q_s, ops_s, x_s, t_s, s_s, bra_w, ket_w, env_sem, p_sem, ops_sem):
-    small = [pltpu.make_async_copy(p, p_s, p_sem), pltpu.make_async_copy(ops, ops_s, ops_sem)]
+    def tensor(j):
+        part = pl.ds(128 * j, 128)
+        return pltpu.make_async_copy(p.at[part], p_s.at[part], p_sem.at[j])
+
+    small = [tensor(0), pltpu.make_async_copy(ops, ops_s, ops_sem)]
     for copy in small:
         copy.start()
 
@@ -66,6 +70,7 @@
 
     for kl in range(8):
         chunk(kl).start(priority=1)
+    tensor(1).start(priority=1)
     low = lax.broadcasted_iota(jnp.int32, (8, 128), 1) < 64
     for copy in small:
         copy.wait()
@@ -146,6 +151,7 @@
             x_s[rows_at((kr * 8 + 8 + k1) * 64 + br * 8, 8), :] = z1
 
     if LATE:
+        tensor(1).wait()
         weights(1)
     sweep(0, put0, turn)
     loop(64 // G, UB, lambda i: bra_group(1, [i * G + g for g in range(G)], [second(i * G + g) for g in range(G)]))
@@ -189,7 +195,7 @@
             pltpu.VMEM((2, 128, 192), BF16),
             pltpu.VMEM((2, 128, 256), BF16),
             pltpu.SemaphoreType.DMA((8,)),
-            pltpu.SemaphoreType.DMA,
+            pltpu.SemaphoreType.DMA((2,)),
             pltpu.SemaphoreType.DMA,
         ],
         compiler_params=pltpu.CompilerParams(vmem_limit_bytes=40 << 20),

time: 65.8 us -> 65.6 us (level)
  no operation moved by 1% of the time
where the time goes in v7:
time: 65.6 us; the launch traced here: 65.4 us
  blocking collectives  55.5 us (85%)
  Pallas kernels  9.32 us (14%)
    all_to_all x1, blocking collectives, body(): merged = lax.all_to_all(blocks, BITS, 0, 0, tiled=True)  41.8 us
    all_to_all x1, blocking collectives, body(): sums = lax.all_to_all(sums, BITS, 0, 0, tiled=True)  13.7 us
    pallas_call x1, Pallas kernels, absorb(): pl.pallas_call(absorb_kernel, out_shape=jax.ShapeDtypeStruct((128, 32, 12...  6.65 us
    pallas_call x1, Pallas kernels, scale(): pl.pallas_call(functools.partial(scale_kernel, entries), out_shape=(jax.S...  1.52 us

profile of v7, /device:TPU:1, one launch (start us, length us, event | category | flops | bytes accessed | tf_op | source)
XLA Modules:
  0.0 65.4 jit_solution(13646948445016794448)
XLA Ops:
  0.6 6.7 %absorb.1 = f32[128,32,128]{2,1,0:T(8,128)S(1)} custom-call(f32[2,1,64,4096]{3,2,1,0:T(8,128)} %env.1, f32[256,8,8]{2,1,0:T(8,128)} %bitcast.7, f32[2,2,2]{2,1,0:T(2,128)} %ops.1), custom_call_target="tpu_custom_call" | custom-call | flops 2147483648 | bytes 4194304 | tf_op jit(solution)/shard_map/absorb/pallas_call | solution.py:182
  7.3 0.0 copy-start
  7.3 41.8 %all_to_all.16.r = f32[128,32,128]{2,1,0:T(8,128)S(1)} all-to-all(f32[128,32,128]{2,1,0:T(8,128)S(1)} %absorb.1), channel_id=1, replica_groups=mesh['bits_0'=4,'bits_1'=4,'bits_2'=4,'bits_3'=2] {'bits_0','bits_1','bi..., dimensions={0} | all-to-all | bytes 4194304 | tf_op jit(solution)/shard_map/all_to_all | solution.py:292
  49.1 0.0 copy-done
  49.1 1.2 %gauge.1 = (f32[2,128,2048]{2,1,0:T(8,128)S(1)}, f32[128,128]{1,0:T(8,128)S(1)}) custom-call(f32[128,32,128]{2,1,0:T(8,128)S(1)} %all_to_all.16.r, f32[128,128]{1,0:T(8,128)S(1)} %copy-done), custom_call_target="tpu_custom_call" | custom-call | flops 536870912 | bytes 4194304 | tf_op jit(solution)/shard_map/gauge/pallas_call | solution.py:238
  50.2 13.7 %all_to_all.17 = f32[128,1,128]{2,1,0:T(1,128)S(1)} all-to-all(f32[128,1,128]{2,1,0:T(1,128)S(1)} %bitcast.6), channel_id=1, replica_groups=mesh['bits_0'=4,'bits_1'=4,'bits_2'=4,'bits_3'=2] {'bits_0','bits_1','bi..., dimensions={0} | all-to-all | bytes 131072 | tf_op jit(solution)/shard_map/all_to_all | solution.py:294
  63.9 1.5 %scale.1 = (f32[2,128,2048]{2,1,0:T(8,128)}, f32[2]{0:T(128)}) custom-call(f32[2,128,2048]{2,1,0:T(8,128)S(1)} %get-tuple-element.4.x, f32[128,128]{1,0:T(8,128)S(1)} %bitcast.5), custom_call_target="tpu_custom_call" | custom-call | flops 524288 | bytes 4194304 | tf_op jit(solution)/shard_map/scale/pallas_call | solution.py:273
Async XLA Ops:
  7.3 41.8 %copy-start = (f32[128,128]{1,0:T(8,128)S(1)}, f32[128,128]{1,0:T(8,128)}, u32[]{:S(2)}) copy-start(f32[128,128]{1,0:T(8,128)} %gm.1) | copy-start | bytes 196612
